TPU v7x, 512 devices: a 8x2x16 block of a 8x8x16 slice. The times are simulated.
512 devices in a mesh: groups: 2 (over y), seg: 32 (over z, core), bin: 8 (over x).
Axes of the slice: x: 8, y: 2, z: 16, core: 2. Of those that a mesh axis runs over, the one named last changes fastest.
The devices are a block of a 8x8x16 slice.
Arguments:
- start_factors: float32 [32768, 128], P(('groups', 'seg', 'bin')), parts along dimension 0, may hold values from -6 to 6
- bin_factors: bfloat16 [16384, 128], P(('groups', 'bin')), parts along dimension 0, may hold values from -0.5 to 0.5
- tile_speed: bfloat16 [64, 8, 12, 128, 128], P(('groups', 'seg'), 'bin'), parts along dimension 0, may hold values from -6 to 6
- tile_weight: bfloat16 [64, 8, 12, 128, 128], P(('groups', 'seg'), 'bin'), parts along dimension 0, may hold values from 0.099609375 to 2
- tile_cells: int32 [64, 8, 12, 2], P(('groups', 'seg'), 'bin'), parts along dimension 0, may hold values from 0 to 7, as said below
- tile_count: int32 [64, 8], P(('groups', 'seg'), 'bin'), parts along dimension 0, may hold values from 1 to 12, as said below
- inner_pairs: int32 [64, 8, 2, 2], P(('groups', 'seg'), 'bin'), parts along dimension 0, may hold values from 0 to 3, as said below
- inner_weight: float32 [64, 8, 2, 128, 128], P(('groups', 'seg'), 'bin'), parts along dimension 0, may hold values from 0 to 0.00390625
- face_rows: int32 [64, 8, 2, 256], P(('groups', 'seg'), 'bin'), parts along dimension 0, may hold values from 0 to 511, as said below
- face_count: int32 [64, 8, 2], P(('groups', 'seg'), 'bin'), parts along dimension 0, may hold values from 128 to 256, as said below
- face_weight: float32 [64, 8, 256, 256], P(('groups', 'seg'), 'bin'), parts along dimension 0, may hold values from 0 to 0.00390625
Outputs:
- solution_factors: float32 [32768, 128], P(('groups', 'seg', 'bin')), parts along dimension 0
- residual: float32 [32768, 128], P(('groups', 'seg', 'bin')), parts along dimension 0
There are 2 independent parts, one for each index of `groups`. A program takes and returns all parts, laid end to end along the dimension named above; each array names one. Nothing has to cross between parts.
Inputs may be any that keep to these rules, and one draw needn't show every extreme that they name: `tile_cells`: the 12 slots of one device name different pairs; the first entry is a segment block of the partition, the second a bin block of the device's bins. `tile_count`: some device of every draw has all 12 slots live. `inner_pairs`: the two blocks of a pair differ; both are segment blocks of the partition. `face_rows`: row numbers within the partition, different within each face list. `face_count`: some face list of every draw has all 256 rows live.
All inputs are finite; a program needn't handle non-finite values.
Results may differ from a plain program's by a relative error of at most 0.0024.
Values sent between devices are 32-bit elements; how exact they have to be, the bound alone decides.
A program may use at most 64 MiB of HBM per device.

v0:
```python
import jax
import jax.numpy as jnp
from jax import lax
from jax.sharding import Mesh
from jax.sharding import PartitionSpec as P

ITERS = 2
SEG = ("seg_0", "seg_1")
SEG_BIN = ("seg_0", "seg_1", "bin")
GROUPS_SEG_BIN = ("groups", "seg_0", "seg_1", "bin")
GROUPS_SEG = ("groups", "seg_0", "seg_1")
highest = lax.Precision.HIGHEST
ridge_weight = 0.5


def from_behind(x, axis, by):
    devices = lax.axis_size(axis)
    pairs = [(i, i + by) for i in range(devices) if 0 <= i + by < devices]
    return lax.ppermute(x, axis, pairs)


def cut_along(x, dim, devices):
    before, after = (x.shape[:dim], x.shape[dim + 1 :])
    return jnp.moveaxis(x.reshape(*before, devices, -1, *after), dim, 0)


def sent_and_summed(x, axis, dim):
    devices = lax.axis_size(axis)
    blocks = lax.all_to_all(cut_along(x, dim, devices), axis, 0, 0, tiled=True)
    return jnp.sum(blocks, axis=0)


def in_order(blocks, dim):
    shape = list(blocks.shape[1:])
    shape[dim] *= blocks.shape[0]
    return jnp.moveaxis(blocks, 0, dim).reshape(shape)


def sent_to_all(x, axis):
    devices = lax.axis_size(axis)
    return lax.all_to_all(jnp.broadcast_to(x[None], (devices, *x.shape)), axis, 0, 0, tiled=True)


def gathered_copies(x, axis, dim):
    return in_order(sent_to_all(x, axis), dim)


def one_axis_at_a_time(x, axes):
    for axis in axes:
        x = lax.psum(x, axis)
    return x


def shards(
    start_factors,
    bin_factors,
    tile_speed,
    tile_weight,
    tile_cells,
    tile_count,
    inner_pairs,
    inner_weight,
    face_rows,
    face_count,
    face_weight,
):
    speeds = tile_speed[0, 0]
    weights = tile_weight[0, 0]
    cells = tile_cells[0, 0]
    n_tiles = speeds.shape[0]
    tile_size = speeds.shape[1]
    own_rows = start_factors.shape[0]
    width = start_factors.shape[1]
    part_rows = own_rows * lax.axis_size("bin")
    part_blocks = part_rows // tile_size
    block_ids = jnp.arange(part_blocks, dtype=jnp.int32)
    live_tiles = (jnp.arange(n_tiles, dtype=jnp.int32) < tile_count[0, 0]).astype(jnp.float32)
    tile_bins = bin_factors.reshape(-1, tile_size, width)[cells[:, 1]]
    bins_wide = tile_bins.astype(jnp.float32)
    tile_gain = weights.astype(jnp.float32) * live_tiles[:, None, None]
    tile_onehot = (cells[:, 0][:, None] == block_ids[None, :]).astype(jnp.float32)
    weighted = (weights.astype(jnp.float32) * speeds.astype(jnp.float32)).astype(jnp.bfloat16)
    rhs_terms = jnp.einsum("kij,kjr->kir", weighted, tile_bins, preferred_element_type=jnp.float32)
    rhs_terms = rhs_terms * live_tiles[:, None, None]
    rhs_part = jnp.einsum("kb,kir->bir", tile_onehot, rhs_terms, precision=highest).reshape(
        part_rows, width
    )
    pairs = inner_pairs[0, 0]
    pair_weight = inner_weight[0, 0]
    left_onehot = (pairs[:, 0][:, None] == block_ids[None, :]).astype(jnp.float32)
    right_onehot = (pairs[:, 1][:, None] == block_ids[None, :]).astype(jnp.float32)
    left_degree = pair_weight.sum(2)
    right_degree = pair_weight.sum(1)
    rows_low = face_rows[0, 0, 0]
    rows_up = face_rows[0, 0, 1]
    face_slots = jnp.arange(rows_low.shape[0], dtype=jnp.int32)
    mask_low = (face_slots < face_count[0, 0, 0]).astype(jnp.float32)
    mask_up = (face_slots < face_count[0, 0, 1]).astype(jnp.float32)
    upper_count = face_count[0, 0, 1:2]
    face_block = face_weight[0, 0]

    def apply_local(whole_rows):
        blocks = whole_rows.reshape(part_blocks, tile_size, width)
        picked = blocks[cells[:, 0]]
        scores = jnp.einsum("kir,kjr->kij", picked, bins_wide, precision=highest) * tile_gain
        pulled = jnp.einsum("kij,kjr->kir", scores, bins_wide, precision=highest)
        left = blocks[pairs[:, 0]]
        right = blocks[pairs[:, 1]]
        to_left = left_degree[..., None] * left - jnp.einsum(
            "kij,kjr->kir", pair_weight, right, precision=highest
        )
        to_right = right_degree[..., None] * right - jnp.einsum(
            "kij,kir->kjr", pair_weight, left, precision=highest
        )
        summed = jnp.einsum("kb,kir->bir", tile_onehot, pulled, precision=highest)
        summed = summed + jnp.einsum("kb,kir->bir", left_onehot, to_left, precision=highest)
        summed = summed + jnp.einsum("kb,kir->bir", right_onehot, to_right, precision=highest)
        summed = summed.reshape(part_rows, width)
        own_face = whole_rows[rows_low] * mask_low[:, None]
        upper_face = whole_rows[rows_up] * mask_up[:, None]
        lower_face, lower_count = from_behind((upper_face, upper_count), SEG, 1)
        lower_mask = (face_slots < lower_count[0]).astype(jnp.float32)
        coupling = face_block * mask_low[:, None] * lower_mask[None, :]
        own_term = coupling.sum(1)[:, None] * own_face - jnp.dot(
            coupling, lower_face, precision=highest
        )
        answer = coupling.sum(0)[:, None] * lower_face - jnp.dot(
            coupling.T, own_face, precision=highest
        )
        returned = from_behind(answer, SEG, -1)
        return summed.at[rows_low].add(own_term).at[rows_up].add(returned)

    def reduce_rows(partial_value):
        reduced = sent_and_summed(partial_value, "bin", 0)
        return reduced

    def spread(vector):
        whole_rows = gathered_copies(vector, "bin", 0)
        return whole_rows

    def fold_sum(values):
        folded = (one_axis_at_a_time(values[0], SEG_BIN), one_axis_at_a_time(values[1], SEG_BIN))
        return folded

    def image_of(vector):
        return reduce_rows(apply_local(spread(vector))) + ridge_weight * vector

    start_whole = gathered_copies(start_factors, "bin", 0)
    residual = reduce_rows(rhs_part - apply_local(start_whole)) - ridge_weight * start_factors
    solution = start_factors
    images = image_of(residual)
    norm_now, product = fold_sum((jnp.sum(residual * residual), jnp.sum(residual * images)))
    step_size = norm_now / product
    direction = residual
    along = images
    for iteration in range(ITERS):
        solution = solution + step_size * direction
        residual = residual - step_size * along
        if iteration + 1 < ITERS:
            images = image_of(residual)
            norm_next, product = fold_sum(
                (jnp.sum(residual * residual), jnp.sum(residual * images))
            )
            beta_ratio = norm_next / norm_now
            step_size = norm_next / (product - beta_ratio * norm_next / step_size)
            direction = residual + beta_ratio * direction
            along = images + beta_ratio * along
            norm_now = norm_next
    outputs = (solution, residual)
    return outputs


def solution(mesh):
    finer = Mesh(
        mesh.devices.reshape(mesh.shape["groups"], 16, 2, mesh.shape["bin"]),
        ("groups", "seg_0", "seg_1", "bin"),
    )
    in_specs = (
        P(GROUPS_SEG_BIN, None),
        P(("groups", "bin"), None),
        P(GROUPS_SEG, "bin", None, None, None),
        P(GROUPS_SEG, "bin", None, None, None),
        P(GROUPS_SEG, "bin", None, None),
        P(GROUPS_SEG, "bin"),
        P(GROUPS_SEG, "bin", None, None),
        P(GROUPS_SEG, "bin", None, None, None),
        P(GROUPS_SEG, "bin", None, None),
        P(GROUPS_SEG, "bin", None),
        P(GROUPS_SEG, "bin", None, None),
    )
    out_specs = (P(GROUPS_SEG_BIN, None), P(GROUPS_SEG_BIN, None))
    return jax.shard_map(
        shards, mesh=finer, in_specs=in_specs, out_specs=out_specs, check_vma=False
    )
```

profile of v0, /device:TPU:80, one launch (start us, length us, event | category | flops | bytes accessed | tf_op | source)
XLA Modules:
  0.0 300.7 jit_solution(3569220163104865625)
XLA Ops:
  0.6 1.5 broadcast_in_dim.6
  2.2 7.4 %all-to-all-start = ((f32[8,64,128]{2,1,0:T(8,128)}), f32[8,64,128]{2,1,0:T(8,128)S(1)}, u32[]{:S(2)}, u32[]{:S(2)}) async-start(f32[8,64,128]{2,1,0:T(8,128)} %broadcast_in_dim.6), calls=%async_computation | async-start | bytes 524288 | tf_op jit(solution)/shard_map/all_to_all | solution.py:41
  10.2 2.2 collective-permute-start
  13.1 0.7 copy-done.28
  13.8 0.8 slice_reduce_fusion
  14.6 0.7 compare_convert_fusion.2
  15.9 0.6 gather_fusion
  17.3 0.9 fusion.9
  18.3 1.3 compare_convert_fusion
  19.7 0.6 compare_convert_fusion.1
  20.4 0.7 fusion.72
  21.6 0.6 gather_fusion.1
  22.2 0.9 convolution_multiply_fusion.3
  25.5 0.7 gather_fusion.5
  26.3 5.6 %collective-permute-start.1 = (f32[256,128]{1,0:T(8,128)S(1)}, f32[256,128]{1,0:T(8,128)S(1)}, u32[]{:S(2)}, u32[]{:S(2)}) collective-permute-start(f32[256,128]{1,0:T(8,128)S(1)} %broadcast_multiply_fusion.2), channel_id=1, source_target_pairs={{0,8},{8,16},{16,24},{24,32},{32,40},{40,48},{48,56},{56,64},{64,7... | collective-permute-start | bytes 393224 | tf_op jit(solution)/shard_map/ppermute | solution.py:19
  32.6 0.9 convolution_add_fusion.2
  34.7 0.7 copy-done.17
  35.3 0.7 gather_fusion.4
  36.1 0.6 copy-done.7
  36.7 0.7 multiply_subtract_fusion.2
  37.4 1.3 collective-permute-start.2
  39.1 2.0 scatter_fusion
  41.2 2.0 scatter_fusion.1
  43.3 17.7 %all_to_all.30 = f32[8,64,128]{2,1,0:T(8,128)S(1)} all-to-all(f32[8,64,128]{2,1,0:T(8,128)S(1)} %bitcast.164), channel_id=1, replica_groups=mesh['groups'=2,'seg_0'=16,'seg_1'=2,'bin'=8] {'bin'}, dimensions={0} | all-to-all | bytes 524288 | tf_op jit(solution)/shard_map/all_to_all | solution.py:29
  61.0 0.7 copy-done.5
  61.8 13.7 %all_to_all.31 = f32[8,64,128]{2,1,0:T(8,128)S(1)} all-to-all(f32[8,64,128]{2,1,0:T(8,128)S(1)} %broadcast_in_dim.7), channel_id=1, replica_groups=mesh['groups'=2,'seg_0'=16,'seg_1'=2,'bin'=8] {'bin'}, dimensions={0} | all-to-all | bytes 524288 | tf_op jit(solution)/shard_map/all_to_all | solution.py:41
  75.5 0.7 gather_fusion.10
  76.2 0.7 gather_fusion.9
  76.9 0.7 gather_fusion.7
  77.6 0.7 gather_fusion.8
  78.3 0.7 gather_fusion.6
  80.5 4.0 %collective-permute-start.3 = (f32[256,128]{1,0:T(8,128)S(1)}, f32[256,128]{1,0:T(8,128)S(1)}, u32[]{:S(2)}, u32[]{:S(2)}) collective-permute-start(f32[256,128]{1,0:T(8,128)S(1)} %broadcast_multiply_fusion.1), channel_id=1, source_target_pairs={{0,8},{8,16},{16,24},{24,32},{32,40},{40,48},{48,56},{56,64},{64,7... | collective-permute-start | bytes 393224 | tf_op jit(solution)/shard_map/ppermute | solution.py:19
  84.5 0.9 convolution_multiply_fusion.2
  86.8 0.9 convolution_add_fusion.1
  88.3 0.7 multiply_subtract_fusion.1
  89.0 1.3 collective-permute-start.4
  90.7 2.0 scatter_fusion.2
  92.8 2.2 collective-permute-done.4
  95.0 2.0 scatter_fusion.3
  97.0 13.9 %all_to_all.32 = f32[8,64,128]{2,1,0:T(8,128)S(1)} all-to-all(f32[8,64,128]{2,1,0:T(8,128)S(1)} %bitcast.163), channel_id=1, replica_groups=mesh['groups'=2,'seg_0'=16,'seg_1'=2,'bin'=8] {'bin'}, dimensions={0} | all-to-all | bytes 524288 | tf_op jit(solution)/shard_map/all_to_all | solution.py:29
  110.9 0.6 multiply_reduce_fusion.2
  111.5 68.4 %all-reduce.1 = (f32[]{:T(128)}, f32[]{:T(128)}) all-reduce(f32[]{:T(128)} %get-tuple-element.9, f32[]{:T(128)} %get-tuple-element.8), channel_id=1, replica_groups=mesh['groups'=2,'seg_0'=16,'seg_1'=2,'bin'=8] {'seg_0'}, use_global_device_ids=true, to_apply=%region_8.0 | all-reduce | flops 2 | bytes 16 | tf_op jit(solution)/shard_map/psum | solution.py:50
  179.9 3.1 %all-reduce.5 = (f32[]{:T(128)}, f32[]{:T(128)}) all-reduce(f32[]{:T(128)} %get-tuple-element.16, f32[]{:T(128)} %get-tuple-element.17), channel_id=1, replica_groups=mesh['groups'=2,'seg_0'=16,'seg_1'=2,'bin'=8] {'seg_1'}, use_global_device_ids=true, to_apply=%region_9.0 | all-reduce | flops 2 | bytes 16 | tf_op jit(solution)/shard_map/psum | solution.py:50
  183.0 15.5 %all-reduce.3 = (f32[]{:T(128)}, f32[]{:T(128)}) all-reduce(f32[]{:T(128)} %get-tuple-element.24, f32[]{:T(128)} %get-tuple-element.25), channel_id=1, replica_groups=mesh['groups'=2,'seg_0'=16,'seg_1'=2,'bin'=8] {'bin'}, use_global_device_ids=true, to_apply=%region_10.0 | all-reduce | flops 2 | bytes 16 | tf_op jit(solution)/shard_map/psum | solution.py:50
  199.9 14.0 %all_to_all.33 = f32[8,64,128]{2,1,0:T(8,128)S(1)} all-to-all(f32[8,64,128]{2,1,0:T(8,128)S(1)} %broadcast_in_dim.8), channel_id=1, replica_groups=mesh['groups'=2,'seg_0'=16,'seg_1'=2,'bin'=8] {'bin'}, dimensions={0} | all-to-all | bytes 524288 | tf_op jit(solution)/shard_map/all_to_all | solution.py:41
  213.9 0.7 gather_fusion.15
  214.7 0.7 gather_fusion.14
  215.4 0.7 gather_fusion.12
  216.1 0.7 gather_fusion.13
  216.8 0.7 gather_fusion.11
  218.3 1.5 collective-permute-start.5
  219.8 0.9 convolution_multiply_fusion.1
  221.8 0.9 convolution_add_fusion
  223.3 0.7 multiply_subtract_fusion
  224.0 1.3 collective-permute-start.6
  225.7 2.0 scatter_fusion.4
  227.8 1.4 collective-permute-done.6
  229.1 2.0 scatter_fusion.5
  231.2 13.3 %all_to_all.34 = f32[8,64,128]{2,1,0:T(8,128)S(1)} all-to-all(f32[8,64,128]{2,1,0:T(8,128)S(1)} %bitcast.160), channel_id=1, replica_groups=mesh['groups'=2,'seg_0'=16,'seg_1'=2,'bin'=8] {'bin'}, dimensions={0} | all-to-all | bytes 524288 | tf_op jit(solution)/shard_map/all_to_all | solution.py:29
  244.5 0.6 multiply_reduce_fusion
  245.1 31.9 %all-reduce = (f32[]{:T(128)}, f32[]{:T(128)}) all-reduce(f32[]{:T(128)} %get-tuple-element.7, f32[]{:T(128)} %get-tuple-element.6), channel_id=1, replica_groups=mesh['groups'=2,'seg_0'=16,'seg_1'=2,'bin'=8] {'seg_0'}, use_global_device_ids=true, to_apply=%region_19.0 | all-reduce | flops 2 | bytes 16 | tf_op jit(solution)/shard_map/psum | solution.py:50
  277.0 3.1 %all-reduce.4 = (f32[]{:T(128)}, f32[]{:T(128)}) all-reduce(f32[]{:T(128)} %get-tuple-element.14, f32[]{:T(128)} %get-tuple-element.15), channel_id=1, replica_groups=mesh['groups'=2,'seg_0'=16,'seg_1'=2,'bin'=8] {'seg_1'}, use_global_device_ids=true, to_apply=%region_20.0 | all-reduce | flops 2 | bytes 16 | tf_op jit(solution)/shard_map/psum | solution.py:50
  280.2 15.4 %all-reduce.2 = (f32[]{:T(128)}, f32[]{:T(128)}) all-reduce(f32[]{:T(128)} %get-tuple-element.22, f32[]{:T(128)} %get-tuple-element.23), channel_id=1, replica_groups=mesh['groups'=2,'seg_0'=16,'seg_1'=2,'bin'=8] {'bin'}, use_global_device_ids=true, to_apply=%region_21.0 | all-reduce | flops 2 | bytes 16 | tf_op jit(solution)/shard_map/psum | solution.py:50
  300.0 0.6 multiply_subtract_fusion.3
  (111 shorter events, 13.8 us)
Async XLA Ops:
  0.6 15.3 %copy-start = (bf16[1024,128]{1,0:T(8,128)(2,1)S(1)}, bf16[1024,128]{1,0:T(8,128)(2,1)}, u32[]{:S(2)}) copy-start(bf16[1024,128]{1,0:T(8,128)(2,1)} %param.12) | copy-start | bytes 786436
  2.2 7.5 %copy-start.30 = (s32[1,1,2]{2,1,0:T(1,128)S(1)}, s32[1,1,2]{2,1,0:T(1,128)}, u32[]{:S(2)}) copy-start(s32[1,1,2]{2,1,0:T(1,128)} %param.20) | copy-start | bytes 28
  2.2 19.4 %all-to-all-start = ((f32[8,64,128]{2,1,0:T(8,128)}), f32[8,64,128]{2,1,0:T(8,128)S(1)}, u32[]{:S(2)}, u32[]{:S(2)}) async-start(f32[8,64,128]{2,1,0:T(8,128)} %broadcast_in_dim.6), calls=%async_computation | async-start | bytes 524288 | tf_op jit(solution)/shard_map/all_to_all | solution.py:41
  10.2 2.2 copy-start.31
  10.2 9.5 %collective-permute-start = (s32[1]{0:T(128)}, s32[1]{0:T(128)}, u32[]{:S(2)}, u32[]{:S(2)}) collective-permute-start(s32[1]{0:T(128)} %bitcast.23), channel_id=1, source_target_pairs={{0,8},{8,16},{16,24},{24,32},{32,40},{40,48},{48,56},{56,64},{64,7... | collective-permute-start | bytes 20 | tf_op jit(solution)/shard_map/ppermute | solution.py:19
  12.4 4.9 %copy-start.12 = (s32[12]{0:T(128)}, s32[12]{0:T(128)S(1)}, u32[]{:S(2)}) copy-start(s32[12]{0:T(128)S(1)} %get-tuple-element.30) | copy-start | bytes 148
  13.1 9.1 %copy-start.20 = (f32[12]{0:T(128)}, f32[12]{0:T(128)S(1)}, u32[]{:S(2)}) copy-start(f32[12]{0:T(128)S(1)} %compare_convert_fusion.3) | copy-start | bytes 148
  13.1 0.7 copy-start.28
  14.6 0.7 copy-start.29
  15.3 10.2 %copy-start.15 = (s32[1024]{0:T(1024)}, s32[1024]{0:T(1024)S(1)}, u32[]{:S(2)}) copy-start(s32[1024]{0:T(1024)S(1)} %pad_clamp_fusion) | copy-start | bytes 12292
  15.9 5.6 %copy-start.25 = (s32[1024]{0:T(1024)}, s32[1024]{0:T(1024)S(1)}, u32[]{:S(2)}) copy-start(s32[1024]{0:T(1024)S(1)} %get-tuple-element.37) | copy-start | bytes 12292
  15.9 1.0 copy-start.3
  15.9 1.1 copy-start.4
  18.2 1.4 copy-start.2
  18.2 2.1 copy-start.1
  18.3 5.3 %copy-start.27 = (s32[1024]{0:T(1024)}, s32[1024]{0:T(1024)S(1)}, u32[]{:S(2)}) copy-start(s32[1024]{0:T(1024)S(1)} %get-tuple-element.36) | copy-start | bytes 12292
  18.3 5.9 %copy-start.26 = (s32[1024]{0:T(1024)}, s32[1024]{0:T(1024)S(1)}, u32[]{:S(2)}) copy-start(s32[1024]{0:T(1024)S(1)} %get-tuple-element.35) | copy-start | bytes 12292
  19.7 5.1 %copy-start.8 = (f32[2,128]{1,0:T(2,128)}, f32[2,128]{1,0:T(2,128)S(1)}, u32[]{:S(2)}) copy-start(f32[2,128]{1,0:T(2,128)S(1)} %get-tuple-element.5) | copy-start | bytes 3076
  19.7 5.3 %copy-start.10 = (f32[2,128]{1,0:T(2,128)}, f32[2,128]{1,0:T(2,128)S(1)}, u32[]{:S(2)}) copy-start(f32[2,128]{1,0:T(2,128)S(1)} %get-tuple-element.4) | copy-start | bytes 3076
  25.5 0.7 copy-start.18
  26.3 5.6 %copy-start.22 = (s32[2]{0:T(128)S(1)}, s32[2]{0:T(128)}, u32[]{:S(2)}) copy-start(s32[2]{0:T(128)} %get-tuple-element.13) | copy-start | bytes 28
  26.3 9.7 %collective-permute-start.1 = (f32[256,128]{1,0:T(8,128)S(1)}, f32[256,128]{1,0:T(8,128)S(1)}, u32[]{:S(2)}, u32[]{:S(2)}) collective-permute-start(f32[256,128]{1,0:T(8,128)S(1)} %broadcast_multiply_fusion.2), channel_id=1, source_target_pairs={{0,8},{8,16},{16,24},{24,32},{32,40},{40,48},{48,56},{56,64},{64,7... | collective-permute-start | bytes 393224 | tf_op jit(solution)/shard_map/ppermute | solution.py:19
  31.9 0.7 copy-start.13
  33.5 0.6 copy-start.24
  34.6 0.7 copy-start.17
  36.0 0.6 copy-start.7
  37.4 1.3 copy-start.6
  37.4 3.8 %collective-permute-start.2 = (f32[256,128]{1,0:T(8,128)S(1)}, f32[256,128]{1,0:T(8,128)S(1)}, u32[]{:S(2)}, u32[]{:S(2)}) collective-permute-start(f32[256,128]{1,0:T(8,128)S(1)} %multiply_subtract_fusion.2), channel_id=1, source_target_pairs={{8,0},{16,8},{24,16},{32,24},{40,32},{48,40},{56,48},{64,56},{72,6... | collective-permute-start | bytes 393224 | tf_op jit(solution)/shard_map/ppermute | solution.py:19
  61.0 0.8 copy-start.5
  61.8 13.7 %copy-start.16 = (s32[1024]{0:T(1024)S(1)}, s32[1024]{0:T(1024)}, u32[]{:S(2)}) copy-start(s32[1024]{0:T(1024)} %copy-done.15) | copy-start | bytes 12292
  78.3 0.7 copy-start.11
  79.1 0.7 copy-start.9
  79.7 0.7 copy-start.19
  80.4 4.1 %copy-start.21 = (f32[12]{0:T(128)S(1)}, f32[12]{0:T(128)}, u32[]{:S(2)}) copy-start(f32[12]{0:T(128)} %copy-done.20) | copy-start | bytes 148
  80.5 7.8 %collective-permute-start.3 = (f32[256,128]{1,0:T(8,128)S(1)}, f32[256,128]{1,0:T(8,128)S(1)}, u32[]{:S(2)}, u32[]{:S(2)}) collective-permute-start(f32[256,128]{1,0:T(8,128)S(1)} %broadcast_multiply_fusion.1), channel_id=1, source_target_pairs={{0,8},{8,16},{16,24},{24,32},{32,40},{40,48},{48,56},{56,64},{64,7... | collective-permute-start | bytes 393224 | tf_op jit(solution)/shard_map/ppermute | solution.py:19
  85.5 0.7 copy-start.23
  86.1 0.7 copy-start.14
  89.0 6.0 %collective-permute-start.4 = (f32[256,128]{1,0:T(8,128)S(1)}, f32[256,128]{1,0:T(8,128)S(1)}, u32[]{:S(2)}, u32[]{:S(2)}) collective-permute-start(f32[256,128]{1,0:T(8,128)S(1)} %multiply_subtract_fusion.1), channel_id=1, source_target_pairs={{8,0},{16,8},{24,16},{32,24},{40,32},{48,40},{56,48},{64,56},{72,6... | collective-permute-start | bytes 393224 | tf_op jit(solution)/shard_map/ppermute | solution.py:19
  218.3 5.0 %collective-permute-start.5 = (f32[256,128]{1,0:T(8,128)S(1)}, f32[256,128]{1,0:T(8,128)S(1)}, u32[]{:S(2)}, u32[]{:S(2)}) collective-permute-start(f32[256,128]{1,0:T(8,128)S(1)} %broadcast_multiply_fusion), channel_id=1, source_target_pairs={{0,8},{8,16},{16,24},{24,32},{32,40},{40,48},{48,56},{56,64},{64,7... | collective-permute-start | bytes 393224 | tf_op jit(solution)/shard_map/ppermute | solution.py:19
  224.0 5.2 %collective-permute-start.6 = (f32[256,128]{1,0:T(8,128)S(1)}, f32[256,128]{1,0:T(8,128)S(1)}, u32[]{:S(2)}, u32[]{:S(2)}) collective-permute-start(f32[256,128]{1,0:T(8,128)S(1)} %multiply_subtract_fusion), channel_id=1, source_target_pairs={{8,0},{16,8},{24,16},{32,24},{40,32},{48,40},{56,48},{64,56},{72,6... | collective-permute-start | bytes 393224 | tf_op jit(solution)/shard_map/ppermute | solution.py:19
where the time goes:
time: 302 us; the launch traced here: 301 us
  blocking collectives  210 us (70%)
  starting transfers between devices  24.7 us (8%)
  other arithmetic  19.4 us (6%)
  local copies, waits for them, and re-layouts  18.1 us (6%)
  matrix products  16.6 us (5%)
  between operations  7.96 us (3%)
  waiting for transfers between devices  3.97 us (1%)
    psum x6, blocking collectives, one_axis_at_a_time(): x = lax.psum(x, axis)  137 us
    all_to_all x3, blocking collectives, sent_and_summed(): blocks = lax.all_to_all(cut_along(x, dim, devices), axis, 0, 0, tiled=True)  44.9 us
    all_to_all x2, blocking collectives, sent_to_all(): lax.all_to_all(jnp.broadcast_to(x[None], (devices, *x.shape)), axis, 0, 0...  27.7 us
    ppermute x7, starting transfers between devices, from_behind(): return lax.ppermute(x, axis, pairs)  17.2 us
    scatter-add x6, other arithmetic, apply_local(): return summed.at[rows_low].add(own_term).at[rows_up].add(returned)  12.3 us
    all_to_all x1, starting transfers between devices, sent_to_all(): lax.all_to_all(jnp.broadcast_to(x[None], (devices, *x.shape)), axis, 0, 0...  7.45 us
  transfers between devices with their start and end apart: 8, of which 3 were waited for; matrix products, arithmetic and copies ran while one was open for 8% of the time, Pallas kernels for 0%

commit v1 on v0

--- a/solution.py
+++ b/solution.py
@@ -47,7 +47,7 @@
 
 def one_axis_at_a_time(x, axes):
     for axis in axes:
-        x = lax.psum(x, axis)
+        x = jnp.sum(lax.all_gather(x, axis), axis=0)
     return x
 
 

time: 302 us -> 327 us (1.083)
  blocking collectives: 210 us -> 176 us
  local copies, waits for them, and re-layouts: 18.1 us -> 38.7 us
  waiting for transfers between devices: 3.97 us -> 20.7 us
  starting transfers between devices: 24.7 us -> 35.5 us
  other arithmetic: 19.4 us -> 30.1 us
    psum x6 -> x0, blocking collectives: 137 us -> none  [one_axis_at_a_time(): x = lax.psum(x, axis)]
    unnamed x0 -> x6, blocking collectives: none -> 135 us
    all_to_all x3 -> x1, blocking collectives: 44.9 us -> 13.3 us  [sent_and_summed(): blocks = lax.all_to_all(cut_along(x, dim, devices), axis, 0, 0, tiled=True)]
    unnamed x64 -> x91, local copies, waits for them, and re-layouts: 4.98 us -> 24.9 us
    all_to_all x0 -> x2, waiting for transfers between devices: none -> 18.7 us  [sent_and_summed(): blocks = lax.all_to_all(cut_along(x, dim, devices), axis, 0, 0, tiled=True)]
    all_to_all x0 -> x2, starting transfers between devices: none -> 10.8 us  [sent_and_summed(): blocks = lax.all_to_all(cut_along(x, dim, devices), axis, 0, 0, tiled=True)]
    reduce_sum x0 -> x12, other arithmetic: none -> 7.28 us  [one_axis_at_a_time(): x = jnp.sum(lax.all_gather(x, axis), axis=0)]
  transfers between devices with their start and end apart: 8 -> 10, of which waited for: 3 -> 5; matrix products, arithmetic and copies ran while one was open for 8% -> 9% of each run, Pallas kernels for 0% -> 0%
where the time goes in v1:
time: 327 us; the launch traced here: 326 us
  blocking collectives  176 us (54%)
  local copies, waits for them, and re-layouts  38.7 us (12%)
  starting transfers between devices  35.5 us (11%)
  other arithmetic  30.1 us (9%)
  waiting for transfers between devices  20.7 us (6%)
  matrix products  16.6 us (5%)
  between operations  7.94 us (2%)
    unnamed x6, blocking collectives  135 us
    all_to_all x2, blocking collectives, sent_to_all(): lax.all_to_all(jnp.broadcast_to(x[None], (devices, *x.shape)), axis, 0, 0...  27.6 us
    unnamed x91, local copies, waits for them, and re-layouts  24.9 us
    all_to_all x2, waiting for transfers between devices, sent_and_summed(): blocks = lax.all_to_all(cut_along(x, dim, devices), axis, 0, 0, tiled=True)  18.7 us
    ppermute x7, starting transfers between devices, from_behind(): return lax.ppermute(x, axis, pairs)  17.2 us
    scatter-add x6, other arithmetic, apply_local(): return summed.at[rows_low].add(own_term).at[rows_up].add(returned)  15 us
    all_to_all x1, blocking collectives, sent_and_summed(): blocks = lax.all_to_all(cut_along(x, dim, devices), axis, 0, 0, tiled=True)  13.3 us
    all_to_all x2, starting transfers between devices, sent_and_summed(): blocks = lax.all_to_all(cut_along(x, dim, devices), axis, 0, 0, tiled=True)  10.8 us
  transfers between devices with their start and end apart: 10, of which 5 were waited for; matrix products, arithmetic and copies ran while one was open for 9% of the time, Pallas kernels for 0%

profile of v1, /device:TPU:80, one launch (start us, length us, event | category | flops | bytes accessed | tf_op | source)
XLA Modules:
  0.0 325.8 jit_solution(2740752290227529239)
XLA Ops:
  0.6 1.5 broadcast_in_dim.6
  2.2 7.4 %all-to-all-start = ((f32[8,64,128]{2,1,0:T(8,128)}), f32[8,64,128]{2,1,0:T(8,128)S(1)}, u32[]{:S(2)}, u32[]{:S(2)}) async-start(f32[8,64,128]{2,1,0:T(8,128)} %broadcast_in_dim.6), calls=%async_computation | async-start | bytes 524288 | tf_op jit(solution)/shard_map/all_to_all | solution.py:41
  10.2 2.2 collective-permute-start
  13.8 0.8 slice_reduce_fusion
  17.3 0.9 fusion.9
  18.3 1.3 compare_convert_fusion
  20.4 0.7 fusion.72
  22.2 0.9 convolution_multiply_fusion.3
  25.5 0.7 gather_fusion.5
  26.3 5.6 %collective-permute-start.1 = (f32[256,128]{1,0:T(8,128)S(1)}, f32[256,128]{1,0:T(8,128)S(1)}, u32[]{:S(2)}, u32[]{:S(2)}) collective-permute-start(f32[256,128]{1,0:T(8,128)S(1)} %broadcast_multiply_fusion.2), channel_id=1, source_target_pairs={{0,8},{8,16},{16,24},{24,32},{32,40},{40,48},{48,56},{56,64},{64,7... | collective-permute-start | bytes 393224 | tf_op jit(solution)/shard_map/ppermute | solution.py:19
  32.6 0.9 convolution_add_fusion.2
  35.3 0.7 gather_fusion.4
  37.4 1.3 collective-permute-start.2
  39.1 2.0 scatter_fusion
  41.2 2.0 scatter_fusion.1
  43.3 0.7 bitcast_subtract_fusion
  44.0 7.2 %all-to-all-start.1 = ((f32[8,64,128]{2,1,0:T(8,128)}), f32[8,64,128]{2,1,0:T(8,128)S(1)}, u32[]{:S(2)}, u32[]{:S(2)}) async-start(f32[8,64,128]{2,1,0:T(8,128)} %bitcast.29), calls=%async_computation.1 | async-start | bytes 524288 | tf_op jit(solution)/shard_map/all_to_all | solution.py:29
  51.2 10.7 %all-to-all-done.1 = f32[8,64,128]{2,1,0:T(8,128)S(1)} async-done(((f32[8,64,128]{2,1,0:T(8,128)}), f32[8,64,128]{2,1,0:T(8,128)S(1)}, u32[]{:S(2)}, u32[]{:S(2)}) %all-to-all-start.1) | async-done | bytes 262176 | tf_op jit(solution)/shard_map/all_to_all | solution.py:29
  62.0 13.7 %all_to_all.30 = f32[8,64,128]{2,1,0:T(8,128)S(1)} all-to-all(f32[8,64,128]{2,1,0:T(8,128)S(1)} %broadcast_in_dim.7), channel_id=1, replica_groups=mesh['groups'=2,'seg_0'=16,'seg_1'=2,'bin'=8] {'bin'}, dimensions={0} | all-to-all | bytes 524288 | tf_op jit(solution)/shard_map/all_to_all | solution.py:41
  75.7 0.7 gather_fusion.10
  76.4 0.7 gather_fusion.9
  78.5 0.7 gather_fusion.6
  80.7 4.0 %collective-permute-start.3 = (f32[256,128]{1,0:T(8,128)S(1)}, f32[256,128]{1,0:T(8,128)S(1)}, u32[]{:S(2)}, u32[]{:S(2)}) collective-permute-start(f32[256,128]{1,0:T(8,128)S(1)} %broadcast_multiply_fusion.1), channel_id=1, source_target_pairs={{0,8},{8,16},{16,24},{24,32},{32,40},{40,48},{48,56},{56,64},{64,7... | collective-permute-start | bytes 393224 | tf_op jit(solution)/shard_map/ppermute | solution.py:19
  84.7 0.9 convolution_multiply_fusion.2
  87.0 0.9 convolution_add_fusion.1
  89.8 1.3 collective-permute-start.4
  91.6 3.4 %scatter_fusion.2 = f32[512,128]{1,0:T(8,128)} fusion(f32[512,128]{1,0:T(8,128)} %bitcast.39, s32[256]{0:T(256)S(1)} %bitcast.183, f32[256,128]{1,0:T(8,128)S(1)} %convolution_subtract_fusion.1), kind=kCustom, calls=%fused_computation.18 | custom fusion | flops 32768 | bytes 394240 | tf_op jit(solution)/shard_map/scatter-add | solution.py:131
  95.0 0.8 collective-permute-done.4
  95.8 3.4 %scatter_fusion.3 = f32[512,128]{1,0:T(8,128)} fusion(f32[512,128]{1,0:T(8,128)} %scatter_fusion.2, s32[256]{0:T(256)S(1)} %bitcast.179, f32[256,128]{1,0:T(8,128)S(1)} %collective-permute-done.4), kind=kCustom, calls=%fused_computation.19 | custom fusion | flops 32768 | bytes 394240 | tf_op jit(solution)/shard_map/scatter-add | solution.py:131
  99.2 3.6 %all-to-all-start.3 = ((f32[8,64,128]{2,1,0:T(8,128)}), f32[8,64,128]{2,1,0:T(8,128)S(1)}, u32[]{:S(2)}, u32[]{:S(2)}) async-start(f32[8,64,128]{2,1,0:T(8,128)} %bitcast.41), calls=%async_computation.3 | async-start | bytes 524288 | tf_op jit(solution)/shard_map/all_to_all | solution.py:29
  102.8 1.3 dynamic-slice
  104.2 1.2 dynamic-slice.1
  105.4 8.0 %all-to-all-done.3 = f32[8,64,128]{2,1,0:T(8,128)S(1)} async-done(((f32[8,64,128]{2,1,0:T(8,128)}), f32[8,64,128]{2,1,0:T(8,128)S(1)}, u32[]{:S(2)}, u32[]{:S(2)}) %all-to-all-start.3) | async-done | bytes 262176 | tf_op jit(solution)/shard_map/all_to_all | solution.py:29
  114.1 1.4 dynamic-update-slice.3
  115.6 1.5 dynamic-update-slice
  117.1 69.0 %all-reduce.13 = (f32[16]{0:T(128)S(1)}, f32[16]{0:T(128)S(1)}) all-reduce(f32[16]{0:T(128)S(1)} %dynamic-update-slice, f32[16]{0:T(128)S(1)} %dynamic-update-slice.3), channel_id=1, replica_groups=mesh['groups'=2,'seg_0'=16,'seg_1'=2,'bin'=8] {'seg_0'}, use_global_device_ids=true, to_apply=%add | all-reduce | flops 32 | bytes 256
  187.3 1.3 dynamic-update-slice.4
  188.6 1.3 dynamic-update-slice.1
  189.9 1.3 dynamic-slice.2
  191.3 2.5 all-reduce.17
  195.0 1.4 dynamic-update-slice.5
  196.3 1.4 dynamic-update-slice.2
  197.8 14.8 %all-reduce.15 = (f32[8]{0:T(128)S(1)}, f32[8]{0:T(128)S(1)}) all-reduce(f32[8]{0:T(128)S(1)} %dynamic-update-slice.2, f32[8]{0:T(128)S(1)} %dynamic-update-slice.5), channel_id=1, replica_groups=mesh['groups'=2,'seg_0'=16,'seg_1'=2,'bin'=8] {'bin'}, use_global_device_ids=true, to_apply=%add.2 | all-reduce | flops 16 | bytes 128
  215.0 13.9 %all_to_all.31 = f32[8,64,128]{2,1,0:T(8,128)S(1)} all-to-all(f32[8,64,128]{2,1,0:T(8,128)S(1)} %broadcast_in_dim.8), channel_id=1, replica_groups=mesh['groups'=2,'seg_0'=16,'seg_1'=2,'bin'=8] {'bin'}, dimensions={0} | all-to-all | bytes 524288 | tf_op jit(solution)/shard_map/all_to_all | solution.py:41
  229.0 0.7 gather_fusion.15
  229.7 0.7 gather_fusion.14
  231.8 0.7 gather_fusion.11
  233.3 1.5 collective-permute-start.5
  234.8 0.9 convolution_multiply_fusion.1
  236.8 0.9 convolution_add_fusion
  239.0 1.3 collective-permute-start.6
  240.7 2.0 scatter_fusion.4
  242.8 0.8 collective-permute-done.6
  243.5 2.0 scatter_fusion.5
  245.6 13.3 %all_to_all.32 = f32[8,64,128]{2,1,0:T(8,128)S(1)} all-to-all(f32[8,64,128]{2,1,0:T(8,128)S(1)} %bitcast.175), channel_id=1, replica_groups=mesh['groups'=2,'seg_0'=16,'seg_1'=2,'bin'=8] {'bin'}, dimensions={0} | all-to-all | bytes 524288 | tf_op jit(solution)/shard_map/all_to_all | solution.py:29
  259.6 1.4 dynamic-update-slice.9
  261.0 1.4 dynamic-update-slice.6
  262.4 31.8 %all-reduce.12 = (f32[16]{0:T(128)S(1)}, f32[16]{0:T(128)S(1)}) all-reduce(f32[16]{0:T(128)S(1)} %dynamic-update-slice.6, f32[16]{0:T(128)S(1)} %dynamic-update-slice.9), channel_id=1, replica_groups=mesh['groups'=2,'seg_0'=16,'seg_1'=2,'bin'=8] {'seg_0'}, use_global_device_ids=true, to_apply=%add.6 | all-reduce | flops 32 | bytes 256
  294.9 1.3 dynamic-update-slice.10
  296.8 1.3 dynamic-update-slice.7
  298.1 2.5 all-reduce.16
  301.2 1.4 dynamic-update-slice.11
  303.2 1.4 dynamic-update-slice.8
  304.6 14.8 %all-reduce.14 = (f32[8]{0:T(128)S(1)}, f32[8]{0:T(128)S(1)}) all-reduce(f32[8]{0:T(128)S(1)} %dynamic-update-slice.8, f32[8]{0:T(128)S(1)} %dynamic-update-slice.11), channel_id=1, replica_groups=mesh['groups'=2,'seg_0'=16,'seg_1'=2,'bin'=8] {'bin'}, use_global_device_ids=true, to_apply=%add.8 | all-reduce | flops 16 | bytes 128
  (152 shorter events, 33.0 us)
Async XLA Ops:
  0.6 15.3 %copy-start = (bf16[1024,128]{1,0:T(8,128)(2,1)S(1)}, bf16[1024,128]{1,0:T(8,128)(2,1)}, u32[]{:S(2)}) copy-start(bf16[1024,128]{1,0:T(8,128)(2,1)} %param.12) | copy-start | bytes 786436
  2.2 7.5 %copy-start.30 = (s32[1,1,2]{2,1,0:T(1,128)S(1)}, s32[1,1,2]{2,1,0:T(1,128)}, u32[]{:S(2)}) copy-start(s32[1,1,2]{2,1,0:T(1,128)} %param.20) | copy-start | bytes 28
  2.2 19.4 %all-to-all-start = ((f32[8,64,128]{2,1,0:T(8,128)}), f32[8,64,128]{2,1,0:T(8,128)S(1)}, u32[]{:S(2)}, u32[]{:S(2)}) async-start(f32[8,64,128]{2,1,0:T(8,128)} %broadcast_in_dim.6), calls=%async_computation | async-start | bytes 524288 | tf_op jit(solution)/shard_map/all_to_all | solution.py:41
  10.2 2.2 copy-start.31
  10.2 9.5 %collective-permute-start = (s32[1]{0:T(128)}, s32[1]{0:T(128)}, u32[]{:S(2)}, u32[]{:S(2)}) collective-permute-start(s32[1]{0:T(128)} %bitcast.23), channel_id=1, source_target_pairs={{0,8},{8,16},{16,24},{24,32},{32,40},{40,48},{48,56},{56,64},{64,7... | collective-permute-start | bytes 20 | tf_op jit(solution)/shard_map/ppermute | solution.py:19
  12.4 4.9 %copy-start.12 = (s32[12]{0:T(128)}, s32[12]{0:T(128)S(1)}, u32[]{:S(2)}) copy-start(s32[12]{0:T(128)S(1)} %get-tuple-element.30) | copy-start | bytes 148
  13.1 9.1 %copy-start.20 = (f32[12]{0:T(128)}, f32[12]{0:T(128)S(1)}, u32[]{:S(2)}) copy-start(f32[12]{0:T(128)S(1)} %compare_convert_fusion.3) | copy-start | bytes 148
  13.1 0.7 copy-start.28
  14.6 0.7 copy-start.29
  15.3 10.2 %copy-start.15 = (s32[1024]{0:T(1024)}, s32[1024]{0:T(1024)S(1)}, u32[]{:S(2)}) copy-start(s32[1024]{0:T(1024)S(1)} %pad_clamp_fusion) | copy-start | bytes 12292
  15.9 5.6 %copy-start.25 = (s32[1024]{0:T(1024)}, s32[1024]{0:T(1024)S(1)}, u32[]{:S(2)}) copy-start(s32[1024]{0:T(1024)S(1)} %get-tuple-element.37) | copy-start | bytes 12292
  15.9 1.0 copy-start.3
  15.9 1.1 copy-start.4
  18.2 1.4 copy-start.2
  18.2 2.1 copy-start.1
  18.3 5.3 %copy-start.27 = (s32[1024]{0:T(1024)}, s32[1024]{0:T(1024)S(1)}, u32[]{:S(2)}) copy-start(s32[1024]{0:T(1024)S(1)} %get-tuple-element.36) | copy-start | bytes 12292
  18.3 5.9 %copy-start.26 = (s32[1024]{0:T(1024)}, s32[1024]{0:T(1024)S(1)}, u32[]{:S(2)}) copy-start(s32[1024]{0:T(1024)S(1)} %get-tuple-element.35) | copy-start | bytes 12292
  19.7 5.1 %copy-start.8 = (f32[2,128]{1,0:T(2,128)}, f32[2,128]{1,0:T(2,128)S(1)}, u32[]{:S(2)}) copy-start(f32[2,128]{1,0:T(2,128)S(1)} %get-tuple-element.5) | copy-start | bytes 3076
  19.7 5.3 %copy-start.10 = (f32[2,128]{1,0:T(2,128)}, f32[2,128]{1,0:T(2,128)S(1)}, u32[]{:S(2)}) copy-start(f32[2,128]{1,0:T(2,128)S(1)} %get-tuple-element.4) | copy-start | bytes 3076
  25.5 0.7 copy-start.18
  26.3 5.6 %copy-start.22 = (s32[2]{0:T(128)S(1)}, s32[2]{0:T(128)}, u32[]{:S(2)}) copy-start(s32[2]{0:T(128)} %get-tuple-element.13) | copy-start | bytes 28
  26.3 9.7 %collective-permute-start.1 = (f32[256,128]{1,0:T(8,128)S(1)}, f32[256,128]{1,0:T(8,128)S(1)}, u32[]{:S(2)}, u32[]{:S(2)}) collective-permute-start(f32[256,128]{1,0:T(8,128)S(1)} %broadcast_multiply_fusion.2), channel_id=1, source_target_pairs={{0,8},{8,16},{16,24},{24,32},{32,40},{40,48},{48,56},{56,64},{64,7... | collective-permute-start | bytes 393224 | tf_op jit(solution)/shard_map/ppermute | solution.py:19
  31.9 0.7 copy-start.13
  33.5 0.6 copy-start.24
  34.6 0.7 copy-start.17
  36.1 0.6 copy-start.7
  37.4 1.3 copy-start.6
  37.4 3.8 %collective-permute-start.2 = (f32[256,128]{1,0:T(8,128)S(1)}, f32[256,128]{1,0:T(8,128)S(1)}, u32[]{:S(2)}, u32[]{:S(2)}) collective-permute-start(f32[256,128]{1,0:T(8,128)S(1)} %multiply_subtract_fusion.2), channel_id=1, source_target_pairs={{8,0},{16,8},{24,16},{32,24},{40,32},{48,40},{56,48},{64,56},{72,6... | collective-permute-start | bytes 393224 | tf_op jit(solution)/shard_map/ppermute | solution.py:19
  44.0 17.9 %all-to-all-start.1 = ((f32[8,64,128]{2,1,0:T(8,128)}), f32[8,64,128]{2,1,0:T(8,128)S(1)}, u32[]{:S(2)}, u32[]{:S(2)}) async-start(f32[8,64,128]{2,1,0:T(8,128)} %bitcast.29), calls=%async_computation.1 | async-start | bytes 524288 | tf_op jit(solution)/shard_map/all_to_all | solution.py:29
  51.2 10.7 %copy-start.5 = (f32[64,128]{1,0:T(8,128)S(1)}, f32[64,128]{1,0:T(8,128)}, u32[]{:S(2)}) copy-start(f32[64,128]{1,0:T(8,128)} %param.11) | copy-start | bytes 98308
  62.0 13.7 %copy-start.16 = (s32[1024]{0:T(1024)S(1)}, s32[1024]{0:T(1024)}, u32[]{:S(2)}) copy-start(s32[1024]{0:T(1024)} %copy-done.15) | copy-start | bytes 12292
  78.5 0.7 copy-start.11
  79.2 0.7 copy-start.9
  79.9 0.7 copy-start.19
  80.6 4.1 %copy-start.21 = (f32[12]{0:T(128)S(1)}, f32[12]{0:T(128)}, u32[]{:S(2)}) copy-start(f32[12]{0:T(128)} %copy-done.20) | copy-start | bytes 148
  80.7 8.4 %collective-permute-start.3 = (f32[256,128]{1,0:T(8,128)S(1)}, f32[256,128]{1,0:T(8,128)S(1)}, u32[]{:S(2)}, u32[]{:S(2)}) collective-permute-start(f32[256,128]{1,0:T(8,128)S(1)} %broadcast_multiply_fusion.1), channel_id=1, source_target_pairs={{0,8},{8,16},{16,24},{24,32},{32,40},{40,48},{48,56},{56,64},{64,7... | collective-permute-start | bytes 393224 | tf_op jit(solution)/shard_map/ppermute | solution.py:19
  85.6 0.7 copy-start.23
  86.3 0.7 copy-start.14
  89.8 6.0 %collective-permute-start.4 = (f32[256,128]{1,0:T(8,128)S(1)}, f32[256,128]{1,0:T(8,128)S(1)}, u32[]{:S(2)}, u32[]{:S(2)}) collective-permute-start(f32[256,128]{1,0:T(8,128)S(1)} %multiply_subtract_fusion.1), channel_id=1, source_target_pairs={{8,0},{16,8},{24,16},{32,24},{40,32},{48,40},{56,48},{64,56},{72,6... | collective-permute-start | bytes 393224 | tf_op jit(solution)/shard_map/ppermute | solution.py:19
  99.2 14.2 %all-to-all-start.3 = ((f32[8,64,128]{2,1,0:T(8,128)}), f32[8,64,128]{2,1,0:T(8,128)S(1)}, u32[]{:S(2)}, u32[]{:S(2)}) async-start(f32[8,64,128]{2,1,0:T(8,128)} %bitcast.41), calls=%async_computation.3 | async-start | bytes 524288 | tf_op jit(solution)/shard_map/all_to_all | solution.py:29
  233.3 5.0 %collective-permute-start.5 = (f32[256,128]{1,0:T(8,128)S(1)}, f32[256,128]{1,0:T(8,128)S(1)}, u32[]{:S(2)}, u32[]{:S(2)}) collective-permute-start(f32[256,128]{1,0:T(8,128)S(1)} %broadcast_multiply_fusion), channel_id=1, source_target_pairs={{0,8},{8,16},{16,24},{24,32},{32,40},{40,48},{48,56},{56,64},{64,7... | collective-permute-start | bytes 393224 | tf_op jit(solution)/shard_map/ppermute | solution.py:19
  239.0 4.6 %collective-permute-start.6 = (f32[256,128]{1,0:T(8,128)S(1)}, f32[256,128]{1,0:T(8,128)S(1)}, u32[]{:S(2)}, u32[]{:S(2)}) collective-permute-start(f32[256,128]{1,0:T(8,128)S(1)} %multiply_subtract_fusion), channel_id=1, source_target_pairs={{8,0},{16,8},{24,16},{32,24},{40,32},{48,40},{56,48},{64,56},{72,6... | collective-permute-start | bytes 393224 | tf_op jit(solution)/shard_map/ppermute | solution.py:19
